TPU v7x, 128 devices: a whole 4x4x4 slice. The times are simulated.
128 devices in a mesh: dp: 4 (over x), fsdp: 32 (over z, y, core).
Axes of the slice: x: 4, y: 4, z: 4, core: 2. Of those that a mesh axis runs over, the one named last changes fastest.
Arguments:
- gradient: bfloat16 [4, 4096, 8, 1024], P('dp', 'fsdp'), may hold values from -3 to 3
- block_owner_index: int32 [32], replicated, may hold values from 0 to 31, as said below
- block_grid_cell: int32 [32], replicated, may hold values from 0 to 31, each once
- left_eigen_basis: float32 [64, 1024, 1024], P('fsdp', None, 'dp'), may hold values from -0.1875 to 0.1875
- right_eigen_basis: float32 [64, 1024, 1024], P('fsdp', None, 'dp'), may hold values from -0.1875 to 0.1875
- left_statistic_matrix: float32 [64, 1024, 1024], P('fsdp', None, 'dp'), may hold values from -6 to 6
- right_statistic_matrix: float32 [64, 1024, 1024], P('fsdp', None, 'dp'), may hold values from -6 to 6
- first_adam_moment: float32 [64, 1024, 1024], P('fsdp', None, 'dp'), may hold values from -0.09 to 0.09
- second_adam_moment: float32 [64, 1024, 1024], P('fsdp', None, 'dp'), may hold values from 1e-05 to 0.001
Outputs:
- new_left_stat: float32 [64, 1024, 1024], P('fsdp', None, 'dp')
- new_right_stat: float32 [64, 1024, 1024], P('fsdp', None, 'dp')
- new_first: float32 [64, 1024, 1024], P('fsdp', None, 'dp')
- new_second: float32 [64, 1024, 1024], P('fsdp', None, 'dp')
- update: bfloat16 [4096, 8, 1024], P('fsdp', None, 'dp')
Inputs may be any that keep to these rules, and one draw needn't show every extreme that they name: `block_owner_index`: no fsdp index owns more than 2 blocks; a quarter of the fsdp indices own 2 blocks and a quarter own none.
All inputs are finite; a program needn't handle non-finite values.
Results may differ from a plain program's by a relative error of at most 0.013.
Values may be sent and summed in bfloat16 or wider, within the bound.
No kernel may reach another device: no remote copies, remote signals or barrier semaphores. Data moves between devices by JAX's collectives and lax.ppermute only.
A program may use at most 128 MiB of HBM per device.

v0:
```python
import jax
import jax.numpy as jnp
from jax import lax
from jax.sharding import PartitionSpec as P


def in_order(blocks, dim):
    blocks = jnp.moveaxis(blocks, 0, dim)
    dims = blocks.shape
    return blocks.reshape(*dims[:dim], dims[dim] * dims[dim + 1], *dims[dim + 2 :])


def on_gathered_pieces(array, axis, dim, work, out_dim):
    width = array.shape[dim]
    pieces = jnp.split(array, 2, axis=dim) if width % 2 == 0 else [array]
    initial = jnp.arange(lax.axis_size(axis)) * width
    blocks = [lax.all_gather(piece, axis) for piece in pieces]
    made = [jax.vmap(work)(b, initial + k * (width // len(pieces))) for k, b in enumerate(blocks)]
    return in_order(jnp.concatenate(made, axis=out_dim + 1), out_dim)


def slot_lookup_table(block_owner_index, block_grid_cell, slot_count, per_owner):
    block_ids = jnp.arange(block_owner_index.shape[0], dtype=jnp.int32)
    shared = (block_owner_index[:, None] == block_owner_index[None, :]) & (
        block_ids[None, :] < block_ids[:, None]
    )
    rank_in = jnp.sum(shared.astype(jnp.int32), axis=1)
    block_slot_index = block_owner_index * per_owner + rank_in
    slot_ids = jnp.arange(slot_count, dtype=jnp.int32)
    matches = (block_slot_index[None, :] == slot_ids[:, None]).astype(jnp.int32)
    filled_marker = jnp.sum(matches, axis=1)
    slot_grid_cell = jnp.sum(matches * block_grid_cell[None, :], axis=1)
    return (block_slot_index, filled_marker, slot_grid_cell)


def local(
    gradient,
    block_owner_index,
    block_grid_cell,
    left_eigen_basis,
    right_eigen_basis,
    left_statistic_matrix,
    right_statistic_matrix,
    first_adam_moment,
    second_adam_moment,
):
    replicas = lax.axis_size("dp")
    members = lax.axis_size("fsdp")
    member = lax.axis_index("fsdp")
    column_group = lax.axis_index("dp")
    per_owner = left_eigen_basis.shape[0]
    block = left_eigen_basis.shape[1]
    width = left_eigen_basis.shape[2]
    band_rows = gradient.shape[1]
    grid_cols = gradient.shape[2]
    bands = block // band_rows
    grid_rows = members // bands
    piece_rows = band_rows // members
    slot_count = per_owner * members
    partial_terms = gradient.reshape(band_rows, grid_cols, replicas, width).astype(jnp.float32)
    reduced = lax.psum_scatter(
        partial_terms.astype(jnp.bfloat16), "dp", scatter_dimension=2, tiled=True
    ).astype(jnp.float32)
    reduced = reduced.reshape(band_rows, grid_cols, width).astype(jnp.bfloat16)
    block_slot_index, filled_marker, slot_grid_cell = slot_lookup_table(
        block_owner_index, block_grid_cell, slot_count, per_owner
    )
    my_filled = lax.dynamic_slice_in_dim(filled_marker, member * per_owner, per_owner, 0)
    split_band = reduced.reshape(members, piece_rows, grid_cols, width)
    received = lax.all_to_all(split_band, "fsdp", split_axis=0, concat_axis=0, tiled=True)
    by_cell = received.reshape(grid_rows, bands, piece_rows, grid_cols, width)
    by_cell = jnp.transpose(by_cell, (0, 3, 1, 2, 4)).reshape(
        grid_rows * grid_cols, bands, piece_rows, width
    )
    leaving = jnp.take(by_cell, slot_grid_cell, axis=0)
    leaving = jnp.where((filled_marker > 0)[:, None, None, None], leaving, jnp.zeros_like(leaving))
    leaving = leaving.reshape(members, per_owner, bands, piece_rows, width)
    landed = lax.all_to_all(leaving, "fsdp", split_axis=0, concat_axis=0, tiled=True)
    col_piece = jnp.transpose(landed, (1, 2, 0, 3, 4)).reshape(per_owner, block, width)
    gathered = lax.all_gather(col_piece, "dp", axis=2, tiled=True)
    row_piece = lax.dynamic_slice_in_dim(gathered, column_group * width, width, 1)
    new_left = 0.95 * left_statistic_matrix + 0.05 * jnp.einsum(
        "sik,sjk->sij", gathered, row_piece, preferred_element_type=jnp.float32
    )
    new_right = 0.95 * right_statistic_matrix + 0.05 * jnp.einsum(
        "ski,skj->sij", gathered, col_piece, preferred_element_type=jnp.float32
    )
    half_turn = jnp.einsum("sik,sij->skj", left_eigen_basis, gathered.astype(jnp.float32)).astype(
        jnp.bfloat16
    )

    def turn_rows(piece, start):
        return jnp.einsum("skj,sjc->skc", piece.astype(jnp.float32), right_eigen_basis)

    turned = on_gathered_pieces(half_turn, "dp", 1, turn_rows, 1)
    new_first = 0.9 * first_adam_moment + 0.1 * turned
    new_second = 0.999 * second_adam_moment + 0.001 * turned * turned
    direction = new_first / (jnp.sqrt(new_second) + 1e-08)
    full_left = lax.all_gather(left_eigen_basis, "dp", axis=2, tiled=True)
    applied = jnp.einsum("sik,skc->sic", full_left, direction)
    piece = right_eigen_basis
    moved = lax.psum_scatter(
        jnp.einsum("sic,sjc->jsi", applied, piece), "dp", scatter_dimension=0, tiled=True
    )
    backward = jnp.transpose(moved.astype(jnp.bfloat16), (1, 2, 0))
    parted = backward.reshape(per_owner, bands, members, piece_rows, width)
    parted = jnp.transpose(parted, (2, 0, 1, 3, 4))
    parted = jnp.where((my_filled > 0)[None, :, None, None, None], parted, jnp.zeros_like(parted))
    homed = lax.all_to_all(parted, "fsdp", split_axis=0, concat_axis=0, tiled=True)
    homed = homed.reshape(slot_count, bands, piece_rows, width)
    all_cells = jnp.arange(grid_rows * grid_cols, dtype=jnp.int32)
    all_hits = (block_grid_cell[None, :] == all_cells[:, None]).astype(jnp.int32)
    cell_slot = jnp.sum(all_hits * block_slot_index[None, :], axis=1)
    per_cell = jnp.take(homed, cell_slot, axis=0).reshape(
        grid_rows, grid_cols, bands, piece_rows, width
    )
    per_cell = jnp.transpose(per_cell, (0, 2, 3, 1, 4)).reshape(
        members, piece_rows, grid_cols, width
    )
    update = lax.all_to_all(per_cell, "fsdp", split_axis=0, concat_axis=0, tiled=True).reshape(
        band_rows, grid_cols, width
    )
    return (new_left, new_right, new_first, new_second, update)


def solution(mesh):
    in_specs = (
        P("dp", "fsdp", None, None),
        P(),
        P(),
        P("fsdp", None, "dp"),
        P("fsdp", None, "dp"),
        P("fsdp", None, "dp"),
        P("fsdp", None, "dp"),
        P("fsdp", None, "dp"),
        P("fsdp", None, "dp"),
    )
    out_specs = (
        P("fsdp", None, "dp"),
        P("fsdp", None, "dp"),
        P("fsdp", None, "dp"),
        P("fsdp", None, "dp"),
        P("fsdp", None, "dp"),
    )
    return jax.shard_map(local, mesh=mesh, in_specs=in_specs, out_specs=out_specs, check_vma=False)
```

profile of v0, /device:TPU:1, one launch (start us, length us, event | category | flops | bytes accessed | tf_op | source)
XLA Modules:
  0.0 404.2 jit_solution(3661794692890048232)
XLA Ops:
  7.2 0.0 copy-start
  7.2 0.0 reduce-scatter.3.cloned.1.call-start
  7.2 3.2 copy.61
  10.4 0.0 reduce-scatter.3.cloned.1.call-update
  10.4 0.6 copy-done.6
  11.1 0.2 convert_reduce_fusion.1
  11.3 0.1 convert_reduce_fusion
  11.4 0.1 reduce_sum.47
  11.5 0.1 gt.22
  11.6 32.2 %reduce-scatter.3.cloned.1.call-done = bf16[128,8,1,256]{3,1,0,2:T(8,128)(2,1)} async-done(((bf16[128,8,4,256]{3,1,0,2:T(8,128)(2,1)}), bf16[128,8,1,256]{3,1,0,2:T(8,128)(2,1)}) %reduce-scatter.3.cloned.1.call-update) | async-done | bytes 524304 | tf_op jit(solution)/shard_map/reduce_scatter | solution.py:61
  43.8 7.8 %all-to-all-start = ((bf16[32,4,8,256]{3,2,1,0:T(8,128)(2,1)}), bf16[32,4,8,256]{3,2,1,0:T(8,128)(2,1)S(1)}, u32[]{:S(2)}, u32[]{:S(2)}) async-start(bf16[32,4,8,256]{3,2,1,0:T(8,128)(2,1)} %bitcast.89), calls=%async_computation.1 | async-start | bytes 1048576 | tf_op jit(solution)/shard_map/all_to_all | solution.py:70
  51.6 0.0 all-gather.7.cloned.1.call-start
  51.7 11.3 %all-to-all-done = bf16[32,4,8,256]{3,2,1,0:T(8,128)(2,1)S(1)} async-done(((bf16[32,4,8,256]{3,2,1,0:T(8,128)(2,1)}), bf16[32,4,8,256]{3,2,1,0:T(8,128)(2,1)S(1)}, u32[]{:S(2)}, u32[]{:S(2)}) %all-to-all-start) | async-done | bytes 524320 | tf_op jit(solution)/shard_map/all_to_all | solution.py:70
  63.0 0.3 copy.62
  63.3 1.6 gather_fusion
  64.9 1.4 select_select_fusion
  66.3 20.7 %all_to_all.20 = bf16[32,2,8,4,256]{4,2,3,1,0:T(8,128)(2,1)S(1)} all-to-all(bf16[32,2,8,4,256]{4,2,3,1,0:T(8,128)(2,1)S(1)} %select_select_fusion), channel_id=1, replica_groups=mesh['dp'=4,'fsdp'=32] {'fsdp'}, dimensions={0} | all-to-all | bytes 2097152 | tf_op jit(solution)/shard_map/all_to_all | solution.py:78
  87.0 0.5 copy.63
  87.5 1.1 reshape.101
  88.6 0.0 all-gather.7.cloned.1.call-update
  88.6 0.0 all-gather.13.cloned.1.call-start
  88.7 46.0 %all-gather.7.cloned.1.call-done = bf16[2,1024,1024]{2,1,0:T(8,128)(2,1)} async-done(((bf16[2,1024,256]{2,1,0:T(8,128)(2,1)}), bf16[2,1024,1024]{2,1,0:T(8,128)(2,1)}) %all-gather.7.cloned.1.call-update) | async-done | bytes 4194320 | tf_op jit(solution)/shard_map/all_gather | solution.py:80
  134.7 4.6 %fusion.16 = bf16[2,256,1024]{1,2,0:T(8,128)(2,1)S(1)} fusion(bf16[2,1024,1024]{2,1,0:T(8,128)(2,1)} %all-gather.7.cloned.1.call-done, f32[2,1024,256]{2,1,0:T(8,128)} %param.12), kind=kOutput, calls=%fused_computation.21 | convolution fusion | flops 1073741824 | bytes 7340032 | tf_op jit(solution)/shard_map/sik,sij->skj/dot_general | solution.py:88
  139.3 0.2 fusion.39
  139.5 1.0 copy.68
  140.5 0.0 all-gather.13.cloned.1.call-update
  140.5 0.0 all-gather.11.cloned.1.call-start
  140.6 1.0 copy.66
  141.6 0.0 all-gather.11.cloned.1.call-update
  141.6 0.0 all-gather.9.cloned.1.call-start
  141.6 2.7 convert.4
  144.3 0.0 all-gather.9.cloned.1.call-update
  144.3 0.0 reduce-scatter.5.cloned.1.call-start
  144.4 29.2 %all-gather.13.cloned.1.call-done = bf16[8,128,1024]{2,1,0:T(8,128)(2,1)} async-done(((bf16[2,128,1024]{2,1,0:T(8,128)(2,1)}), bf16[8,128,1024]{2,1,0:T(8,128)(2,1)}) %all-gather.13.cloned.1.call-update) | async-done | bytes 2097168 | tf_op jit(solution)/shard_map/all_gather | solution.py:17
  173.6 2.3 fusion.22
  175.9 30.6 %all-gather.11.cloned.1.call-done = bf16[8,128,1024]{2,1,0:T(8,128)(2,1)} async-done(((bf16[2,128,1024]{2,1,0:T(8,128)(2,1)}), bf16[8,128,1024]{2,1,0:T(8,128)(2,1)}) %all-gather.11.cloned.1.call-update) | async-done | bytes 2097168 | tf_op jit(solution)/shard_map/all_gather | solution.py:17
  206.5 2.3 fusion.17
  208.8 0.0 copy-start.3
  208.8 0.0 copy-start.4
  208.8 0.1 pad_maximum_fusion
  208.9 1.4 copy-done.3
  210.4 0.6 copy-done.4
  211.0 2.6 fusion
  213.6 45.1 %all-gather.9.cloned.1.call-done = bf16[2,1024,1024]{2,1,0:T(8,128)(2,1)} async-done(((bf16[2,1024,256]{2,1,0:T(8,128)(2,1)}), bf16[2,1024,1024]{2,1,0:T(8,128)(2,1)}) %all-gather.9.cloned.1.call-update) | async-done | bytes 4194320 | tf_op jit(solution)/shard_map/all_gather | solution.py:99
  258.7 9.2 %convolution_bitcast_fusion = f32[1024,2,1024]{0,2,1:T(8,128)} fusion(f32[2,1024,256]{2,1,0:T(8,128)S(1)} %copy-done, bf16[2,1024,1024]{2,1,0:T(8,128)(2,1)} %all-gather.9.cloned.1.call-done, f32[2,1024,256]{2,1,0:T(8,128)} %get-tuple-element.18, f32[2,1024,256]{2,1,0:T(8,128)} %get-tuple-element.19), kind=kOutput, calls=%fused_computation.2 | convolution fusion | flops 2148532224 | bytes 18874368 | tf_op jit(solution)/shard_map/sic,sjc->jsi/dot_general | solution.py:103
  267.9 0.0 reduce-scatter.5.cloned.1.call-update
  268.0 0.1 select_reduce_fusion
  268.1 0.1 reduce_sum.50
  268.2 0.1 dynamic-slice_compare_fusion
  268.2 82.6 %reduce-scatter.5.cloned.1.call-done = f32[256,2,1024]{0,2,1:T(8,128)} async-done(((f32[1024,2,1024]{0,2,1:T(8,128)}), f32[256,2,1024]{0,2,1:T(8,128)}) %reduce-scatter.5.cloned.1.call-update) | async-done | bytes 2097168 | tf_op jit(solution)/shard_map/reduce_scatter | solution.py:102
  350.9 1.7 convert_bitcast_fusion
  352.6 0.3 reshape.103
  352.9 0.0 copy-start.2
  352.9 1.6 fusion.27
  354.5 7.8 %all-to-all-start.2 = ((bf16[32,2,8,4,256]{4,2,3,1,0:T(8,128)(2,1)}), bf16[32,2,8,4,256]{4,2,3,1,0:T(8,128)(2,1)S(1)}, u32[]{:S(2)}, u32[]{:S(2)}) async-start(bf16[32,2,8,4,256]{4,2,3,1,0:T(8,128)(2,1)} %fusion.27), calls=%async_computation.4 | async-start | bytes 2097152 | tf_op jit(solution)/shard_map/all_to_all | solution.py:109
  362.3 5.9 %multiply_add_fusion = f32[2,1024,256]{2,1,0:T(8,128)} fusion(f32[2,1024,256]{2,1,0:T(8,128)} %param.15, bf16[2,1024,1024]{2,1,0:T(8,128)(2,1)} %all-gather.7.cloned.1.call-done, bf16[2,1024,256]{2,1,0:T(8,128)(2,1)S(1)} %copy-done.2), kind=kOutput, calls=%fused_computation.18 | convolution fusion | flops 1075314688 | bytes 9437184 | tf_op jit(solution)/shard_map/ski,skj->sij/dot_general | solution.py:85
  368.2 11.1 %all-to-all-done.2 = bf16[32,2,8,4,256]{4,2,3,1,0:T(8,128)(2,1)S(1)} async-done(((bf16[32,2,8,4,256]{4,2,3,1,0:T(8,128)(2,1)}), bf16[32,2,8,4,256]{4,2,3,1,0:T(8,128)(2,1)S(1)}, u32[]{:S(2)}, u32[]{:S(2)}) %all-to-all-start.2) | async-done | bytes 1048608 | tf_op jit(solution)/shard_map/all_to_all | solution.py:109
  379.3 0.6 gather_fusion.1
  379.9 0.1 select_bitcast_fusion
  380.0 1.1 copy.73
  381.1 3.9 all-to-all-start.3
  385.0 6.0 %multiply_add_fusion.1 = f32[2,1024,256]{2,1,0:T(8,128)} fusion(f32[2,1024,256]{2,1,0:T(8,128)} %param.14, bf16[2,1024,1024]{2,1,0:T(8,128)(2,1)} %all-gather.7.cloned.1.call-done, s32[]{:T(128)S(6)} %select_n.66), kind=kOutput, calls=%fused_computation.19 | convolution fusion | flops 1075314688 | bytes 9437188 | tf_op jit(solution)/shard_map/sik,sjk->sij/dot_general | solution.py:82
  391.0 5.5 %all-to-all-done.3 = bf16[32,4,8,256]{3,2,1,0:T(8,128)(2,1)S(1)} async-done(((bf16[32,4,8,256]{3,2,1,0:T(8,128)(2,1)}), bf16[32,4,8,256]{3,2,1,0:T(8,128)(2,1)S(1)}, u32[]{:S(2)}, u32[]{:S(2)}) %all-to-all-start.3) | async-done | bytes 524320 | tf_op jit(solution)/shard_map/all_to_all | solution.py:120
  396.6 0.8 copy.91
  (15 shorter events, 0.1 us)
Async XLA Ops:
  7.2 166.4 %copy-start = (f32[2,1024,256]{2,1,0:T(8,128)S(1)}, f32[2,1024,256]{2,1,0:T(8,128)}, u32[]{:S(2)}) copy-start(f32[2,1024,256]{2,1,0:T(8,128)} %param.13) | copy-start | bytes 6291460
  7.2 36.6 %reduce-scatter.3.cloned.1.call-start = ((), (), s32[]{:S(2)}) async-start(), calls=%async_computation.6 | async-start | bytes 2621440 | tf_op jit(solution)/shard_map/reduce_scatter | solution.py:61
  10.4 0.7 copy-start.6
  10.4 0.8 copy-start.5
  43.8 19.2 %all-to-all-start = ((bf16[32,4,8,256]{3,2,1,0:T(8,128)(2,1)}), bf16[32,4,8,256]{3,2,1,0:T(8,128)(2,1)S(1)}, u32[]{:S(2)}, u32[]{:S(2)}) async-start(bf16[32,4,8,256]{3,2,1,0:T(8,128)(2,1)} %bitcast.89), calls=%async_computation.1 | async-start | bytes 1048576 | tf_op jit(solution)/shard_map/all_to_all | solution.py:70
  51.6 83.1 %all-gather.7.cloned.1.call-start = ((), (), s32[]{:S(2)}) async-start(), calls=%async_computation.7 | async-start | bytes 5242880 | tf_op jit(solution)/shard_map/all_gather | solution.py:80
  88.6 84.9 %all-gather.13.cloned.1.call-start = ((), (), s32[]{:S(2)}) async-start(), calls=%async_computation.11 | async-start | bytes 2621440 | tf_op jit(solution)/shard_map/all_gather | solution.py:17
  140.5 66.0 %all-gather.11.cloned.1.call-start = ((), (), s32[]{:S(2)}) async-start(), calls=%async_computation.10 | async-start | bytes 2621440 | tf_op jit(solution)/shard_map/all_gather | solution.py:17
  141.6 117.2 %all-gather.9.cloned.1.call-start = ((), (), s32[]{:S(2)}) async-start(), calls=%async_computation.8 | async-start | bytes 5242880 | tf_op jit(solution)/shard_map/all_gather | solution.py:99
  144.3 206.5 %reduce-scatter.5.cloned.1.call-start = ((), (), s32[]{:S(2)}) async-start(), calls=%async_computation.9 | async-start | bytes 10485760 | tf_op jit(solution)/shard_map/reduce_scatter | solution.py:102
  208.8 1.6 copy-start.3
  208.8 2.2 copy-start.4
  352.9 9.4 %copy-start.2 = (bf16[2,1024,256]{2,1,0:T(8,128)(2,1)S(1)}, bf16[2,1024,256]{2,1,0:T(8,128)(2,1)}, u32[]{:S(2)}) copy-start(bf16[2,1024,256]{2,1,0:T(8,128)(2,1)} %reshape.101) | copy-start | bytes 3145732
  354.5 24.8 %all-to-all-start.2 = ((bf16[32,2,8,4,256]{4,2,3,1,0:T(8,128)(2,1)}), bf16[32,2,8,4,256]{4,2,3,1,0:T(8,128)(2,1)S(1)}, u32[]{:S(2)}, u32[]{:S(2)}) async-start(bf16[32,2,8,4,256]{4,2,3,1,0:T(8,128)(2,1)} %fusion.27), calls=%async_computation.4 | async-start | bytes 2097152 | tf_op jit(solution)/shard_map/all_to_all | solution.py:109
  381.1 15.5 %all-to-all-start.3 = ((bf16[32,4,8,256]{3,2,1,0:T(8,128)(2,1)}), bf16[32,4,8,256]{3,2,1,0:T(8,128)(2,1)S(1)}, u32[]{:S(2)}, u32[]{:S(2)}) async-start(bf16[32,4,8,256]{3,2,1,0:T(8,128)(2,1)} %bitcast.28), calls=%async_computation.5 | async-start | bytes 1048576 | tf_op jit(solution)/shard_map/all_to_all | solution.py:120
  385.0 12.3 %copy-start.1 = (f32[2,1024,256]{2,1,0:T(8,128)S(1)}, f32[2,1024,256]{2,1,0:T(8,128)}, u32[]{:S(2)}) copy-start(f32[2,1024,256]{2,1,0:T(8,128)} %param.13) | copy-start | bytes 6291460
Sparse Core Ops, SparseCore 0:
  11.0 32.7 reduce-scatter.2
  88.8 45.8 all-gather.6
  140.6 32.8 all-gather.12
  175.6 30.7 all-gather.10
  208.5 50.1 all-gather.8
  268.1 82.7 reduce-scatter.4
where the time goes:
time: 405 us; the launch traced here: 404 us
  waiting for transfers between devices  294 us (73%)
  matrix products  30.3 us (7%)
  blocking collectives  20.7 us (5%)
  starting transfers between devices  19.7 us (5%)
  local copies, waits for them, and re-layouts  14.6 us (4%)
  between operations  14.3 us (4%)
  other arithmetic  10.8 us (3%)
    reduce_scatter x1, waiting for transfers between devices, local(): lax.psum_scatter(jnp.einsum('sic,sjc->jsi', applied, piece), 'dp', scatte...  82.6 us
    all_gather x2, waiting for transfers between devices, on_gathered_pieces(): blocks = [lax.all_gather(piece, axis) for piece in pieces]  59.8 us
    all_gather x1, waiting for transfers between devices, local(): gathered = lax.all_gather(col_piece, 'dp', axis=2, tiled=True)  46 us
    all_gather x1, waiting for transfers between devices, local(): full_left = lax.all_gather(left_eigen_basis, 'dp', axis=2, tiled=True)  45.1 us
    reduce_scatter x1, waiting for transfers between devices, local(): lax.psum_scatter(partial_terms.astype(jnp.bfloat16), 'dp', scatter_dimens...  32.2 us
    all_to_all x1, blocking collectives, local(): lax.all_to_all(leaving, 'fsdp', split_axis=0, concat_axis=0, tiled=True)  20.7 us
    all_to_all x1, waiting for transfers between devices, local(): lax.all_to_all(split_band, 'fsdp', split_axis=0, concat_axis=0, tiled=True)  11.3 us
    all_to_all x1, waiting for transfers between devices, local(): lax.all_to_all(parted, 'fsdp', split_axis=0, concat_axis=0, tiled=True)  11.1 us
  transfers between devices with their start and end apart: 9, of which 9 were waited for; matrix products, arithmetic and copies ran while one was open for 6% of the time, Pallas kernels for 0%

commit v1 on v0

--- a/solution.py
+++ b/solution.py
@@ -96,7 +96,8 @@
     new_first = 0.9 * first_adam_moment + 0.1 * turned
     new_second = 0.999 * second_adam_moment + 0.001 * turned * turned
     direction = new_first / (jnp.sqrt(new_second) + 1e-08)
-    full_left = lax.all_gather(left_eigen_basis, "dp", axis=2, tiled=True)
+    parts = lax.all_gather(left_eigen_basis, "dp")
+    full_left = jnp.concatenate(parts, axis=2)
     applied = jnp.einsum("sik,skc->sic", full_left, direction)
     piece = right_eigen_basis
     moved = lax.psum_scatter(

time: 405 us -> 405 us (level)
  waiting for transfers between devices: 294 us -> 287 us
  local copies, waits for them, and re-layouts: 14.6 us -> 20.9 us
    reshape x0 -> x1, local copies, waits for them, and re-layouts: none -> 6.29 us  [local(): full_left = jnp.concatenate(parts, axis=2)]
  transfers between devices with their start and end apart: 9 -> 9, of which waited for: 9 -> 9; matrix products, arithmetic and copies ran while one was open for 6% -> 8% of each run, Pallas kernels for 0% -> 0%
where the time goes in v1:
time: 405 us; the launch traced here: 404 us
  waiting for transfers between devices  287 us (71%)
  matrix products  30.6 us (8%)
  local copies, waits for them, and re-layouts  20.9 us (5%)
  blocking collectives  20.7 us (5%)
  starting transfers between devices  19.7 us (5%)
  between operations  14.3 us (4%)
  other arithmetic  10.8 us (3%)
    reduce_scatter x1, waiting for transfers between devices, local(): lax.psum_scatter(jnp.einsum('sic,sjc->jsi', applied, piece), 'dp', scatte...  80.5 us
    all_gather x2, waiting for transfers between devices, on_gathered_pieces(): blocks = [lax.all_gather(piece, axis) for piece in pieces]  57.5 us
    all_gather x1, waiting for transfers between devices, local(): parts = lax.all_gather(left_eigen_basis, 'dp')  45.6 us
    all_gather x1, waiting for transfers between devices, local(): gathered = lax.all_gather(col_piece, 'dp', axis=2, tiled=True)  43.2 us
    reduce_scatter x1, waiting for transfers between devices, local(): lax.psum_scatter(partial_terms.astype(jnp.bfloat16), 'dp', scatter_dimens...  32.2 us
    all_to_all x1, blocking collectives, local(): lax.all_to_all(leaving, 'fsdp', split_axis=0, concat_axis=0, tiled=True)  20.7 us
    all_to_all x1, waiting for transfers between devices, local(): lax.all_to_all(split_band, 'fsdp', split_axis=0, concat_axis=0, tiled=True)  11.3 us
    all_to_all x1, waiting for transfers between devices, local(): lax.all_to_all(parted, 'fsdp', split_axis=0, concat_axis=0, tiled=True)  11.1 us
  transfers between devices with their start and end apart: 9, of which 9 were waited for; matrix products, arithmetic and copies ran while one was open for 8% of the time, Pallas kernels for 0%

profile of v1, /device:TPU:1, one launch (start us, length us, event | category | flops | bytes accessed | tf_op | source)
XLA Modules:
  0.0 404.1 jit_solution(12529445119142255741)
XLA Ops:
  7.2 0.0 copy-start
  7.2 0.0 reduce-scatter.3.cloned.1.call-start
  7.2 3.2 copy.67
  10.4 0.0 reduce-scatter.3.cloned.1.call-update
  10.4 0.6 copy-done.6
  11.1 0.2 convert_reduce_fusion.1
  11.3 0.1 convert_reduce_fusion
  11.4 0.1 reduce_sum.47
  11.5 0.1 gt.22
  11.6 32.2 %reduce-scatter.3.cloned.1.call-done = bf16[128,8,1,256]{3,1,0,2:T(8,128)(2,1)} async-done(((bf16[128,8,4,256]{3,1,0,2:T(8,128)(2,1)}), bf16[128,8,1,256]{3,1,0,2:T(8,128)(2,1)}) %reduce-scatter.3.cloned.1.call-update) | async-done | bytes 524304 | tf_op jit(solution)/shard_map/reduce_scatter | solution.py:61
  43.8 7.8 %all-to-all-start = ((bf16[32,4,8,256]{3,2,1,0:T(8,128)(2,1)}), bf16[32,4,8,256]{3,2,1,0:T(8,128)(2,1)S(1)}, u32[]{:S(2)}, u32[]{:S(2)}) async-start(bf16[32,4,8,256]{3,2,1,0:T(8,128)(2,1)} %bitcast.95), calls=%async_computation.1 | async-start | bytes 1048576 | tf_op jit(solution)/shard_map/all_to_all | solution.py:70
  51.6 0.0 all-gather.8.cloned.1.call-start
  51.7 11.3 %all-to-all-done = bf16[32,4,8,256]{3,2,1,0:T(8,128)(2,1)S(1)} async-done(((bf16[32,4,8,256]{3,2,1,0:T(8,128)(2,1)}), bf16[32,4,8,256]{3,2,1,0:T(8,128)(2,1)S(1)}, u32[]{:S(2)}, u32[]{:S(2)}) %all-to-all-start) | async-done | bytes 524320 | tf_op jit(solution)/shard_map/all_to_all | solution.py:70
  63.0 0.3 copy.68
  63.3 1.6 gather_fusion
  64.9 1.4 select_select_fusion
  66.3 20.7 %all_to_all.20 = bf16[32,2,8,4,256]{4,2,3,1,0:T(8,128)(2,1)S(1)} all-to-all(bf16[32,2,8,4,256]{4,2,3,1,0:T(8,128)(2,1)S(1)} %select_select_fusion), channel_id=1, replica_groups=mesh['dp'=4,'fsdp'=32] {'fsdp'}, dimensions={0} | all-to-all | bytes 2097152 | tf_op jit(solution)/shard_map/all_to_all | solution.py:78
  87.0 0.5 copy.69
  87.5 1.1 reshape.107
  88.6 0.0 all-gather.8.cloned.1.call-update
  88.6 0.0 all-gather.14.cloned.1.call-start
  88.7 2.7 convert.4
  91.4 0.0 all-gather.14.cloned.1.call-update
  91.4 0.0 all-gather.12.cloned.1.call-start
  91.4 43.2 %all-gather.8.cloned.1.call-done = bf16[2,1024,1024]{2,1,0:T(8,128)(2,1)} async-done(((bf16[2,1024,256]{2,1,0:T(8,128)(2,1)}), bf16[2,1024,1024]{2,1,0:T(8,128)(2,1)}) %all-gather.8.cloned.1.call-update) | async-done | bytes 4194320 | tf_op jit(solution)/shard_map/all_gather | solution.py:80
  134.7 4.6 %fusion.16 = bf16[2,256,1024]{1,2,0:T(8,128)(2,1)S(1)} fusion(bf16[2,1024,1024]{2,1,0:T(8,128)(2,1)} %all-gather.8.cloned.1.call-done, f32[2,1024,256]{2,1,0:T(8,128)} %param.12), kind=kOutput, calls=%fused_computation.21 | convolution fusion | flops 1073741824 | bytes 7340032 | tf_op jit(solution)/shard_map/sik,sij->skj/dot_general | solution.py:88
  139.3 0.2 fusion.39
  139.5 1.0 copy.74
  140.5 0.0 all-gather.12.cloned.1.call-update
  140.5 0.0 all-gather.10.cloned.1.call-start
  140.6 1.0 copy.72
  141.6 0.0 all-gather.10.cloned.1.call-update
  141.6 0.0 reduce-scatter.5.cloned.1.call-start
  141.6 45.6 %all-gather.14.cloned.1.call-done = bf16[8,1024,256]{2,1,0:T(8,128)(2,1)} async-done(((bf16[2,1024,256]{2,1,0:T(8,128)(2,1)}), bf16[8,1024,256]{2,1,0:T(8,128)(2,1)}) %all-gather.14.cloned.1.call-update) | async-done | bytes 4194320 | tf_op jit(solution)/shard_map/all_gather | solution.py:99
  187.3 6.3 %copy.76 = bf16[2,1024,4,256]{1,3,2,0:T(8,128)(2,1)} copy(bf16[2,1024,4,256]{3,1,0,2:T(8,128)(2,1)} %bitcast.86) | data formatting | bytes 8388608 | tf_op jit(solution)/shard_map/reshape | solution.py:100
  193.6 26.9 %all-gather.12.cloned.1.call-done = bf16[8,128,1024]{2,1,0:T(8,128)(2,1)} async-done(((bf16[2,128,1024]{2,1,0:T(8,128)(2,1)}), bf16[8,128,1024]{2,1,0:T(8,128)(2,1)}) %all-gather.12.cloned.1.call-update) | async-done | bytes 2097168 | tf_op jit(solution)/shard_map/all_gather | solution.py:17
  220.5 2.3 fusion.22
  222.8 30.6 %all-gather.10.cloned.1.call-done = bf16[8,128,1024]{2,1,0:T(8,128)(2,1)} async-done(((bf16[2,128,1024]{2,1,0:T(8,128)(2,1)}), bf16[8,128,1024]{2,1,0:T(8,128)(2,1)}) %all-gather.10.cloned.1.call-update) | async-done | bytes 2097168 | tf_op jit(solution)/shard_map/all_gather | solution.py:17
  253.4 2.3 fusion.17
  255.7 0.0 copy-start.3
  255.7 0.0 copy-start.4
  255.7 0.1 pad_maximum_fusion
  255.9 1.4 copy-done.3
  257.3 0.6 copy-done.4
  257.9 2.6 fusion
  260.6 9.4 %convolution_bitcast_fusion = f32[1024,2,1024]{0,2,1:T(8,128)} fusion(f32[2,1024,256]{2,1,0:T(8,128)S(1)} %copy-done, bf16[2,1024,1024]{1,2,0:T(8,128)(2,1)} %bitcast.83, f32[2,1024,256]{2,1,0:T(8,128)} %get-tuple-element.18, f32[2,1024,256]{2,1,0:T(8,128)} %get-tuple-element.19), kind=kOutput, calls=%fused_computation.2 | convolution fusion | flops 2148532224 | bytes 18874368 | tf_op jit(solution)/shard_map/sic,sjc->jsi/dot_general | solution.py:104
  270.0 0.0 reduce-scatter.5.cloned.1.call-update
  270.0 0.1 select_reduce_fusion
  270.1 0.1 reduce_sum.50
  270.2 0.1 dynamic-slice_compare_fusion
  270.3 80.5 %reduce-scatter.5.cloned.1.call-done = f32[256,2,1024]{0,2,1:T(8,128)} async-done(((f32[1024,2,1024]{0,2,1:T(8,128)}), f32[256,2,1024]{0,2,1:T(8,128)}) %reduce-scatter.5.cloned.1.call-update) | async-done | bytes 2097168 | tf_op jit(solution)/shard_map/reduce_scatter | solution.py:103
  350.8 1.7 convert_bitcast_fusion
  352.5 0.3 reshape.111
  352.8 1.6 fusion.27
  354.4 7.8 %all-to-all-start.2 = ((bf16[32,2,8,4,256]{4,2,3,1,0:T(8,128)(2,1)}), bf16[32,2,8,4,256]{4,2,3,1,0:T(8,128)(2,1)S(1)}, u32[]{:S(2)}, u32[]{:S(2)}) async-start(bf16[32,2,8,4,256]{4,2,3,1,0:T(8,128)(2,1)} %fusion.27), calls=%async_computation.4 | async-start | bytes 2097152 | tf_op jit(solution)/shard_map/all_to_all | solution.py:110
  362.2 5.9 %multiply_add_fusion = f32[2,1024,256]{2,1,0:T(8,128)} fusion(f32[2,1024,256]{2,1,0:T(8,128)} %param.15, bf16[2,1024,1024]{2,1,0:T(8,128)(2,1)} %all-gather.8.cloned.1.call-done, bf16[2,1024,256]{2,1,0:T(8,128)(2,1)S(1)} %copy-done.2), kind=kOutput, calls=%fused_computation.18 | convolution fusion | flops 1075314688 | bytes 9437184 | tf_op jit(solution)/shard_map/ski,skj->sij/dot_general | solution.py:85
  368.1 11.1 %all-to-all-done.2 = bf16[32,2,8,4,256]{4,2,3,1,0:T(8,128)(2,1)S(1)} async-done(((bf16[32,2,8,4,256]{4,2,3,1,0:T(8,128)(2,1)}), bf16[32,2,8,4,256]{4,2,3,1,0:T(8,128)(2,1)S(1)}, u32[]{:S(2)}, u32[]{:S(2)}) %all-to-all-start.2) | async-done | bytes 1048608 | tf_op jit(solution)/shard_map/all_to_all | solution.py:110
  379.2 0.6 gather_fusion.1
  379.8 0.1 select_bitcast_fusion
  379.9 1.1 copy.81
  381.0 3.9 all-to-all-start.3
  385.0 6.0 %multiply_add_fusion.1 = f32[2,1024,256]{2,1,0:T(8,128)} fusion(f32[2,1024,256]{2,1,0:T(8,128)} %param.14, bf16[2,1024,1024]{2,1,0:T(8,128)(2,1)} %all-gather.8.cloned.1.call-done, s32[]{:T(128)S(6)} %select_n.66), kind=kOutput, calls=%fused_computation.19 | convolution fusion | flops 1075314688 | bytes 9437188 | tf_op jit(solution)/shard_map/sik,sjk->sij/dot_general | solution.py:82
  391.0 5.5 %all-to-all-done.3 = bf16[32,4,8,256]{3,2,1,0:T(8,128)(2,1)S(1)} async-done(((bf16[32,4,8,256]{3,2,1,0:T(8,128)(2,1)}), bf16[32,4,8,256]{3,2,1,0:T(8,128)(2,1)S(1)}, u32[]{:S(2)}, u32[]{:S(2)}) %all-to-all-start.3) | async-done | bytes 524320 | tf_op jit(solution)/shard_map/all_to_all | solution.py:121
  396.5 0.8 copy.100
  (16 shorter events, 0.1 us)
Async XLA Ops:
  7.2 213.3 %copy-start = (f32[2,1024,256]{2,1,0:T(8,128)S(1)}, f32[2,1024,256]{2,1,0:T(8,128)}, u32[]{:S(2)}) copy-start(f32[2,1024,256]{2,1,0:T(8,128)} %param.13) | copy-start | bytes 6291460
  7.2 36.6 %reduce-scatter.3.cloned.1.call-start = ((), (), s32[]{:S(2)}) async-start(), calls=%async_computation.6 | async-start | bytes 2621440 | tf_op jit(solution)/shard_map/reduce_scatter | solution.py:61
  10.4 0.7 copy-start.6
  10.4 0.8 copy-start.5
  43.8 19.2 %all-to-all-start = ((bf16[32,4,8,256]{3,2,1,0:T(8,128)(2,1)}), bf16[32,4,8,256]{3,2,1,0:T(8,128)(2,1)S(1)}, u32[]{:S(2)}, u32[]{:S(2)}) async-start(bf16[32,4,8,256]{3,2,1,0:T(8,128)(2,1)} %bitcast.95), calls=%async_computation.1 | async-start | bytes 1048576 | tf_op jit(solution)/shard_map/all_to_all | solution.py:70
  51.6 83.1 %all-gather.8.cloned.1.call-start = ((), (), s32[]{:S(2)}) async-start(), calls=%async_computation.7 | async-start | bytes 5242880 | tf_op jit(solution)/shard_map/all_gather | solution.py:80
  88.6 98.6 %all-gather.14.cloned.1.call-start = ((), (), s32[]{:S(2)}) async-start(), calls=%async_computation.11 | async-start | bytes 5242880 | tf_op jit(solution)/shard_map/all_gather | solution.py:99
  91.4 129.1 %all-gather.12.cloned.1.call-start = ((), (), s32[]{:S(2)}) async-start(), calls=%async_computation.10 | async-start | bytes 2621440 | tf_op jit(solution)/shard_map/all_gather | solution.py:17
  140.5 112.9 %all-gather.10.cloned.1.call-start = ((), (), s32[]{:S(2)}) async-start(), calls=%async_computation.9 | async-start | bytes 2621440 | tf_op jit(solution)/shard_map/all_gather | solution.py:17
  141.6 209.2 %reduce-scatter.5.cloned.1.call-start = ((), (), s32[]{:S(2)}) async-start(), calls=%async_computation.8 | async-start | bytes 10485760 | tf_op jit(solution)/shard_map/reduce_scatter | solution.py:103
  255.7 1.6 copy-start.3
  255.7 2.2 copy-start.4
  352.8 9.4 %copy-start.2 = (bf16[2,1024,256]{2,1,0:T(8,128)(2,1)S(1)}, bf16[2,1024,256]{2,1,0:T(8,128)(2,1)}, u32[]{:S(2)}) copy-start(bf16[2,1024,256]{2,1,0:T(8,128)(2,1)} %reshape.107) | copy-start | bytes 3145732
  354.4 24.8 %all-to-all-start.2 = ((bf16[32,2,8,4,256]{4,2,3,1,0:T(8,128)(2,1)}), bf16[32,2,8,4,256]{4,2,3,1,0:T(8,128)(2,1)S(1)}, u32[]{:S(2)}, u32[]{:S(2)}) async-start(bf16[32,2,8,4,256]{4,2,3,1,0:T(8,128)(2,1)} %fusion.27), calls=%async_computation.4 | async-start | bytes 2097152 | tf_op jit(solution)/shard_map/all_to_all | solution.py:110
  381.0 15.5 %all-to-all-start.3 = ((bf16[32,4,8,256]{3,2,1,0:T(8,128)(2,1)}), bf16[32,4,8,256]{3,2,1,0:T(8,128)(2,1)S(1)}, u32[]{:S(2)}, u32[]{:S(2)}) async-start(bf16[32,4,8,256]{3,2,1,0:T(8,128)(2,1)} %bitcast.31), calls=%async_computation.5 | async-start | bytes 1048576 | tf_op jit(solution)/shard_map/all_to_all | solution.py:121
  385.0 12.3 %copy-start.1 = (f32[2,1024,256]{2,1,0:T(8,128)S(1)}, f32[2,1024,256]{2,1,0:T(8,128)}, u32[]{:S(2)}) copy-start(f32[2,1024,256]{2,1,0:T(8,128)} %param.13) | copy-start | bytes 6291460
Sparse Core Ops, SparseCore 0:
  11.0 32.7 reduce-scatter.2
  88.8 45.8 all-gather.7
  136.9 50.3 all-gather.13
  189.4 31.0 all-gather.11
  222.6 30.7 all-gather.9
  270.1 80.6 reduce-scatter.4
